TPU v7x, 32 devices: a whole 2x2x4 slice. The times are simulated.
32 devices in a mesh: rows: 8 (over z, x), grp: 4 (over y, core).
Axes of the slice: x: 2, y: 2, z: 4, core: 2. Of those that a mesh axis runs over, the one named last changes fastest.
Arguments:
- matrix: bfloat16 [10240, 16384], P(('rows', 'grp')), may hold values from -36 to 36
- sample_rows: int32 [32, 128, 256], P(('rows', 'grp')), may hold values from 0 to 319
- pair_list: int32 [8, 8, 4], replicated, may hold values from 0 to 255, as said below
- pair_count: int32 [8, 8], replicated, may hold values from 1 to 4, as said below
- pair_blocks: int32 [256, 2], replicated, may hold values from 0 to 127, as said below
Outputs:
- gram: float32 [256, 128, 128], P(('rows', 'grp'))
Inputs may be any that keep to these rules, and one draw needn't show every extreme that they name: `pair_list`: entry [s, r, k] lies in [r * 32, (r + 1) * 32); the 4 entries of one [s, r] are distinct. `pair_count`: every row group has some owner with all 4 slots active, and some owner has all 4 slots active from every row group. `pair_blocks`: the two blocks of a pair differ.
All inputs are finite; a program needn't handle non-finite values.
Results may differ from a plain program's by a relative error of at most 0.0016.
Values sent between devices are 32-bit elements; how exact they have to be, the bound alone decides.
No kernel may reach another device: no remote copies, remote signals or barrier semaphores. Data moves between devices by JAX's collectives and lax.ppermute only.
A program may use at most 192 MiB of HBM per device.

v0:
```python
import math
import jax
import jax.numpy as jnp
from jax import lax
from jax.sharding import PartitionSpec as P

epsilon = 1e-06


def shards(matrix, sample_rows, pair_list, pair_count, pair_blocks):
    rows_dev, column_count = matrix.shape
    block_count = sample_rows.shape[1]
    sample_count = sample_rows.shape[2]
    width = column_count // block_count
    row_axis_size = lax.axis_size("rows")
    grp_axis_size = lax.axis_size("grp")
    slot_cap = pair_list.shape[2]
    region_size = pair_blocks.shape[0] // row_axis_size
    row_index = lax.axis_index("rows")
    grp_index = lax.axis_index("grp")
    squares = jnp.sum(jnp.square(matrix.astype(jnp.float32)), axis=0)
    column_total = lax.psum(squares, ("rows", "grp"))
    root_mean = jnp.sqrt(column_total / (rows_dev * row_axis_size * grp_axis_size) + epsilon)
    positions = lax.iota(jnp.int32, rows_dev)
    picked = sample_rows[0]
    multiplicity = jnp.sum(
        (picked[:, :, None] == positions[None, None, :]).astype(jnp.float32), axis=1
    )
    blocks = matrix.reshape(rows_dev, block_count, width)
    weighted = (jnp.transpose(multiplicity)[:, :, None] * blocks.astype(jnp.float32)).astype(
        jnp.bfloat16
    )
    my_pairs = pair_list[row_index]
    my_counts = pair_count[row_index]
    live_mask = (lax.iota(jnp.int32, slot_cap)[None, :] < my_counts[:, None]).astype(jnp.float32)
    pair_ids = my_pairs.reshape(-1)
    slot_total = pair_ids.shape[0]
    group_size = math.gcd(32, slot_total)
    first_block = jnp.take(pair_blocks[:, 0], pair_ids).reshape(-1, group_size)
    second_block = jnp.take(pair_blocks[:, 1], pair_ids).reshape(-1, group_size)

    def tile_group(block_pair):
        weighted_cols = jnp.take(weighted, block_pair[0], axis=1)
        plain_cols = jnp.take(blocks, block_pair[1], axis=1)
        return jnp.einsum(
            "rgi,rgj->gij", weighted_cols, plain_cols, preferred_element_type=jnp.float32
        )

    partial_tiles = lax.map(tile_group, (first_block, second_block))
    partial_tiles = (
        partial_tiles.reshape(row_axis_size, slot_cap, width, width) * live_mask[:, :, None, None]
    )
    received = lax.all_to_all(partial_tiles, "rows", split_axis=0, concat_axis=0, tiled=True)
    source_ids = pair_list[:, row_index, :]
    local_ids = source_ids.reshape(-1) - row_index * region_size
    select_matrix = (lax.iota(jnp.int32, region_size)[:, None] == local_ids[None, :]).astype(
        jnp.float32
    )
    flat_received = received.reshape(local_ids.shape[0], width * width)
    owner_tiles = jnp.dot(
        select_matrix,
        flat_received,
        precision=lax.Precision.HIGHEST,
        preferred_element_type=jnp.float32,
    )
    owned_tiles = lax.psum_scatter(
        owner_tiles.reshape(region_size, width, width), "grp", scatter_dimension=0, tiled=True
    )
    tile_dev = owned_tiles.shape[0]
    owned_pairs = (row_index * grp_axis_size + grp_index) * tile_dev + lax.iota(jnp.int32, tile_dev)
    owned_blocks = jnp.take(pair_blocks, owned_pairs, axis=0)
    scale_blocks = root_mean.reshape(block_count, width)
    left_scale = jnp.take(scale_blocks, owned_blocks[:, 0], axis=0)
    right_scale = jnp.take(scale_blocks, owned_blocks[:, 1], axis=0)
    return owned_tiles / (sample_count * left_scale[:, :, None] * right_scale[:, None, :])


def solution(mesh):
    in_specs = (P(("rows", "grp"), None), P(("rows", "grp"), None, None), P(), P(), P())
    out_specs = P(("rows", "grp"), None, None)
    return jax.shard_map(shards, mesh=mesh, in_specs=in_specs, out_specs=out_specs, check_vma=False)
```

profile of v0, /device:TPU:1, one launch (start us, length us, event | category | flops | bytes accessed | tf_op | source)
XLA Modules:
  0.0 226.1 jit_solution(7144208598119614567)
XLA Ops:
  7.4 0.0 copy-start
  7.4 0.7 constant_dynamic-slice_fusion.1
  8.1 0.1 copy.22
  8.2 0.1 reshape_squeeze.4
  8.2 0.8 fusion.18
  9.0 0.7 gather_fusion.1
  9.7 0.7 gather_fusion.3
  10.4 9.4 %convert_reduce_fusion = f32[128,320]{1,0:T(8,128)S(1)} fusion(s32[128,256]{1,0:T(8,128)} %bitcast.48), kind=kLoop, calls=%fused_computation.7 | loop fusion | flops 31416320 | bytes 294912 | tf_op jit(solution)/shard_map/reduce_sum | solution.py:26
  19.8 11.0 %copy_bitcast_fusion = bf16[320,128,128]{2,0,1:T(8,128)(2,1)} fusion(bf16[320,16384]{1,0:T(8,128)(2,1)} %param.11), kind=kLoop, calls=%fused_computation.11 | loop fusion | bytes 20971520 | tf_op jit(solution)/shard_map/reshape | solution.py:29
  30.8 10.0 %multiply_convert_fusion = bf16[320,128,128]{2,0,1:T(8,128)(2,1)} fusion(f32[320,128]{0,1:T(8,128)S(1)} %bitcast.47, bf16[320,16384]{1,0:T(8,128)(2,1)} %param.11), kind=kLoop, calls=%fused_computation.10 | loop fusion | flops 15728640 | bytes 21135360 | tf_op jit(solution)/shard_map/convert_element_type | solution.py:30
  40.8 0.0 copy-done
  40.8 0.1 fusion.14
  40.9 5.0 %gather_fusion.2 = bf16[32,320,128]{2,1,0:T(8,128)(2,1)S(1)} fusion(bf16[320,128,128]{2,0,1:T(8,128)(2,1)} %multiply_convert_fusion, s32[1024]{0:T(1024)S(1)} %get-tuple-element.39), kind=kCustom, calls=%fused_computation.1.clone | custom fusion | bytes 5243008 | tf_op jit(solution)/shard_map/while/body/eval_jaxpr/jit(_take)/gather | solution.py:43
  45.9 6.4 %gather_fusion.4 = bf16[32,320,128]{2,1,0:T(8,128)(2,1)} fusion(bf16[320,128,128]{2,0,1:T(8,128)(2,1)} %copy_bitcast_fusion, s32[1024]{0:T(1024)S(1)} %get-tuple-element.38), kind=kCustom, calls=%fused_computation.4.clone | custom fusion | bytes 5243008 | tf_op jit(solution)/shard_map/while/body/eval_jaxpr/jit(_take)/gather | solution.py:44
  52.3 3.0 %fusion = f32[32,128,128]{2,1,0:T(8,128)S(1)} fusion(bf16[32,320,128]{2,1,0:T(8,128)(2,1)} %gather_fusion.4, bf16[32,320,128]{2,1,0:T(8,128)(2,1)S(1)} %gather_fusion.2, pred[32]{0:T(512)(128)(4,1)S(1)} %get-tuple-element.34, pred[32]{0:T(512)(128)(4,1)S(1)} %get-tuple-element.28), kind=kOutput, calls=%fused_computation.12 | convolution fusion | flops 338165760 | bytes 7340096 | tf_op jit(solution)/shard_map/while/body/eval_jaxpr/rgi,rgj->gij/dot_general | solution.py:45
  55.3 1.6 broadcast_multiply_fusion
  56.9 6.3 %all-to-all-start = ((f32[8,4,128,128]{3,2,1,0:T(8,128)}), f32[8,4,128,128]{3,2,1,0:T(8,128)S(1)}, u32[]{:S(2)}, u32[]{:S(2)}) async-start(f32[8,4,128,128]{3,2,1,0:T(8,128)} %broadcast_multiply_fusion), calls=%async_computation | async-start | bytes 4194304 | tf_op jit(solution)/shard_map/all_to_all | solution.py:53
  63.2 0.0 copy-start.1
  63.2 0.0 all-reduce.2.cloned.1.call-start
  63.3 6.8 %multiply_reduce_fusion = f32[16384]{0:T(1024)} fusion(bf16[320,16384]{1,0:T(8,128)(2,1)} %param.11), kind=kLoop, calls=%fused_computation.9 | loop fusion | flops 15712256 | bytes 10551296 | tf_op jit(solution)/shard_map/reduce_sum | solution.py:21
  70.0 0.0 all-reduce.2.cloned.1.call-update
  70.0 0.2 reduce-scatter.2.cloned.1.call-start
  70.3 0.0 copy-done.1
  70.3 0.3 subtract_reduce_fusion
  70.6 0.1 sub.15
  70.7 40.5 %all-to-all-done = f32[8,4,128,128]{3,2,1,0:T(8,128)S(1)} async-done(((f32[8,4,128,128]{3,2,1,0:T(8,128)}), f32[8,4,128,128]{3,2,1,0:T(8,128)S(1)}, u32[]{:S(2)}, u32[]{:S(2)}) %all-to-all-start) | async-done | bytes 2097184 | tf_op jit(solution)/shard_map/all_to_all | solution.py:53
  111.2 0.0 copy-start.2
  111.2 3.8 %fusion.7 = f32[32,128,128]{2,0,1:T(8,128)} fusion(s32[32]{0:T(128)S(1)} %sub.15, f32[4,8,128,128]{3,2,1,0:T(8,128)S(1)} %bitcast.45), kind=kOutput, calls=%fused_computation.20 | convolution fusion | flops 201327616 | bytes 4194432 | tf_op jit(solution)/shard_map/dot_general | solution.py:60
  114.9 0.0 reduce-scatter.2.cloned.1.call-update
  115.0 0.0 copy-done.2
  115.0 0.1 copy.26
  115.2 0.6 gather_fusion
  115.7 0.1 broadcast_select_fusion.1
  115.8 0.2 slice_reduce_fusion.1
  116.1 98.2 %all-reduce.2.cloned.1.call-done = f32[16384]{0:T(1024)} async-done(((f32[16384]{0:T(1024)}), f32[16384]{0:T(1024)}) %all-reduce.2.cloned.1.call-update) | async-done | bytes 65552 | tf_op jit(solution)/shard_map/psum | solution.py:22
  214.2 0.9 sqrt_bitcast_fusion
  215.1 0.6 gather_fusion.5
  215.7 0.1 select_multiply_fusion
  215.7 0.1 copy.27
  215.8 0.6 gather_fusion.6
  216.4 0.1 broadcast_select_fusion
  216.5 0.0 reduce-scatter.2.cloned.1.call-done
  216.5 1.2 multiply_divide_fusion
  217.7 0.9 copy.28
  (13 shorter events, 0.1 us)
Async XLA Ops:
  7.4 33.4 %copy-start = (s32[8,8]{1,0:T(8,128)S(1)}, s32[8,8]{1,0:T(8,128)}, u32[]{:S(2)}) copy-start(s32[8,8]{1,0:T(8,128)} %param.14) | copy-start | bytes 772
  56.9 54.3 %all-to-all-start = ((f32[8,4,128,128]{3,2,1,0:T(8,128)}), f32[8,4,128,128]{3,2,1,0:T(8,128)S(1)}, u32[]{:S(2)}, u32[]{:S(2)}) async-start(f32[8,4,128,128]{3,2,1,0:T(8,128)} %broadcast_multiply_fusion), calls=%async_computation | async-start | bytes 4194304 | tf_op jit(solution)/shard_map/all_to_all | solution.py:53
  63.2 7.1 %copy-start.1 = (s32[8,8,4]{1,2,0:T(4,128)S(1)}, s32[8,8,4]{1,2,0:T(4,128)}, u32[]{:S(2)}) copy-start(s32[8,8,4]{1,2,0:T(4,128)} %param.13) | copy-start | bytes 3076
  63.2 151.0 %all-reduce.2.cloned.1.call-start = ((), (), s32[]{:S(2)}) async-start(), calls=%async_computation.3 | async-start | bytes 131072 | tf_op jit(solution)/shard_map/psum | solution.py:22
  70.0 146.4 %reduce-scatter.2.cloned.1.call-start = ((), (), s32[]{:S(2)}) async-start(), calls=%async_computation.2 | async-start | bytes 2621440 | tf_op jit(solution)/shard_map/reduce_scatter | solution.py:66
  111.2 3.8 %copy-start.2 = (s32[256,2]{0,1:T(2,128)S(1)}, s32[256,2]{0,1:T(2,128)}, u32[]{:S(2)}) copy-start(s32[256,2]{0,1:T(2,128)} %param.15) | copy-start | bytes 6148
Sparse Core Ops, SparseCore 0:
  70.2 144.0 all-reduce.1
Sparse Core Ops, SparseCore 1:
  115.1 31.1 reduce-scatter.1
where the time goes:
time: 227 us; the launch traced here: 226 us
  waiting for transfers between devices  139 us (61%)
  other arithmetic  30.4 us (13%)
  local copies, waits for them, and re-layouts  28.5 us (13%)
  between operations  15 us (7%)
  matrix products  6.79 us (3%)
  starting transfers between devices  6.61 us (3%)
    psum x1, waiting for transfers between devices, shards(): column_total = lax.psum(squares, ('rows', 'grp'))  98.2 us
    all_to_all x1, waiting for transfers between devices, shards(): lax.all_to_all(partial_tiles, 'rows', split_axis=0, concat_axis=0, tiled=...  40.5 us
    reshape x1, local copies, waits for them, and re-layouts, shards(): blocks = matrix.reshape(rows_dev, block_count, width)  11 us
    convert_element_type x1, other arithmetic, shards(): (jnp.transpose(multiplicity)[:, :, None] * blocks.astype(jnp.float32)).as...  10 us
    reduce_sum x1, other arithmetic, shards(): jnp.sum((picked[:, :, None] == positions[None, None, :]).astype(jnp.float...  9.36 us
    reduce_sum x1, other arithmetic, shards(): squares = jnp.sum(jnp.square(matrix.astype(jnp.float32)), axis=0)  6.75 us
    gather x1, local copies, waits for them, and re-layouts, tile_group(): plain_cols = jnp.take(blocks, block_pair[1], axis=1)  6.38 us
    all_to_all x1, starting transfers between devices, shards(): lax.all_to_all(partial_tiles, 'rows', split_axis=0, concat_axis=0, tiled=...  6.34 us
  transfers between devices with their start and end apart: 3, of which 2 were waited for; matrix products, arithmetic and copies ran while one was open for 6% of the time, Pallas kernels for 0%

commit v1 on v0

--- a/solution.py
+++ b/solution.py
@@ -8,6 +8,10 @@
 
 
 def shards(matrix, sample_rows, pair_list, pair_count, pair_blocks):
+
+    def scan_members_all(original):
+        return lax.all_gather(original, axis_name=("rows", "grp")).sum(axis=0)
+
     rows_dev, column_count = matrix.shape
     block_count = sample_rows.shape[1]
     sample_count = sample_rows.shape[2]
@@ -19,7 +23,7 @@
     row_index = lax.axis_index("rows")
     grp_index = lax.axis_index("grp")
     squares = jnp.sum(jnp.square(matrix.astype(jnp.float32)), axis=0)
-    column_total = lax.psum(squares, ("rows", "grp"))
+    column_total = scan_members_all(squares)
     root_mean = jnp.sqrt(column_total / (rows_dev * row_axis_size * grp_axis_size) + epsilon)
     positions = lax.iota(jnp.int32, rows_dev)
     picked = sample_rows[0]

time: 227 us -> 161 us (0.71)
  waiting for transfers between devices: 139 us -> 73.6 us
    psum x1 -> x0, waiting for transfers between devices: 98.2 us -> none  [shards(): column_total = lax.psum(squares, ('rows', 'grp'))]
    reduce_scatter x1, waiting for transfers between devices: 0.01 us -> 26.7 us  [shards(): lax.psum_scatter(owner_tiles.reshape(region_size, width, width), 'grp', s...]
    all_to_all x1, waiting for transfers between devices: 40.5 us -> 46.9 us  [shards(): lax.all_to_all(partial_tiles, 'rows', split_axis=0, concat_axis=0, tiled=...]
  transfers between devices with their start and end apart: 3 -> 3, of which waited for: 2 -> 2; matrix products, arithmetic and copies ran while one was open for 6% -> 35% of each run, Pallas kernels for 0% -> 0%
where the time goes in v1:
time: 161 us; the launch traced here: 160 us
  waiting for transfers between devices  73.6 us (46%)
  local copies, waits for them, and re-layouts  28.8 us (18%)
  other arithmetic  28.8 us (18%)
  between operations  15.1 us (9%)
  matrix products  7.05 us (4%)
  starting transfers between devices  6.32 us (4%)
    all_to_all x1, waiting for transfers between devices, shards(): lax.all_to_all(partial_tiles, 'rows', split_axis=0, concat_axis=0, tiled=...  46.9 us
    reduce_scatter x1, waiting for transfers between devices, shards(): lax.psum_scatter(owner_tiles.reshape(region_size, width, width), 'grp', s...  26.7 us
    reshape x1, local copies, waits for them, and re-layouts, shards(): blocks = matrix.reshape(rows_dev, block_count, width)  11 us
    convert_element_type x1, other arithmetic, shards(): (jnp.transpose(multiplicity)[:, :, None] * blocks.astype(jnp.float32)).as...  9.97 us
    reduce_sum x1, other arithmetic, shards(): jnp.sum((picked[:, :, None] == positions[None, None, :]).astype(jnp.float...  8.39 us
    reduce_sum x1, other arithmetic, shards(): squares = jnp.sum(jnp.square(matrix.astype(jnp.float32)), axis=0)  6.76 us
    gather x1, local copies, waits for them, and re-layouts, tile_group(): plain_cols = jnp.take(blocks, block_pair[1], axis=1)  6.38 us
    all_to_all x1, starting transfers between devices, shards(): lax.all_to_all(partial_tiles, 'rows', split_axis=0, concat_axis=0, tiled=...  6.09 us
  transfers between devices with their start and end apart: 3, of which 2 were waited for; matrix products, arithmetic and copies ran while one was open for 35% of the time, Pallas kernels for 0%

profile of v1, /device:TPU:1, one launch (start us, length us, event | category | flops | bytes accessed | tf_op | source)
XLA Modules:
  0.0 159.7 jit_solution(10268728227132983596)
XLA Ops:
  7.4 0.0 copy-start
  7.4 0.0 all-gather.3.cloned.1.call-start
  7.4 6.8 %multiply_reduce_fusion = f32[16384]{0:T(1024)} fusion(bf16[320,16384]{1,0:T(8,128)(2,1)} %param.11), kind=kLoop, calls=%fused_computation.9 | loop fusion | flops 15712256 | bytes 10551296 | tf_op jit(solution)/shard_map/reduce_sum | solution.py:25
  14.1 0.0 all-gather.3.cloned.1.call-update
  14.2 0.0 copy-start.2
  14.2 0.0 copy-start.3
  14.2 0.0 copy-start.1
  14.2 11.0 %copy_bitcast_fusion = bf16[320,128,128]{2,0,1:T(8,128)(2,1)} fusion(bf16[320,16384]{1,0:T(8,128)(2,1)} %param.11), kind=kLoop, calls=%fused_computation.11 | loop fusion | bytes 20971520 | tf_op jit(solution)/shard_map/reshape | solution.py:33
  25.2 0.0 copy-done.2
  25.2 0.1 copy.29
  25.3 0.1 reshape_squeeze.4
  25.4 0.0 copy-done.3
  25.4 0.7 gather_fusion.1
  26.1 0.7 gather_fusion.3
  26.8 0.0 copy-done.1
  26.8 8.4 %convert_reduce_fusion = f32[128,320]{1,0:T(8,128)S(1)} fusion(s32[128,256]{1,0:T(8,128)S(1)} %bitcast.48), kind=kLoop, calls=%fused_computation.7 | loop fusion | flops 31416320 | bytes 294912 | tf_op jit(solution)/shard_map/reduce_sum | solution.py:30
  35.2 10.0 %multiply_convert_fusion = bf16[320,128,128]{2,0,1:T(8,128)(2,1)} fusion(f32[320,128]{0,1:T(8,128)S(1)} %bitcast.47, bf16[320,16384]{1,0:T(8,128)(2,1)} %param.11), kind=kLoop, calls=%fused_computation.10 | loop fusion | flops 15728640 | bytes 21135360 | tf_op jit(solution)/shard_map/convert_element_type | solution.py:34
  45.2 0.0 copy-done
  45.2 0.1 fusion.14
  45.3 5.0 %gather_fusion.2 = bf16[32,320,128]{2,1,0:T(8,128)(2,1)S(1)} fusion(bf16[320,128,128]{2,0,1:T(8,128)(2,1)} %multiply_convert_fusion, s32[1024]{0:T(1024)S(1)} %get-tuple-element.39), kind=kCustom, calls=%fused_computation.1.clone | custom fusion | bytes 5243008 | tf_op jit(solution)/shard_map/while/body/eval_jaxpr/jit(_take)/gather | solution.py:47
  50.4 6.4 %gather_fusion.4 = bf16[32,320,128]{2,1,0:T(8,128)(2,1)} fusion(bf16[320,128,128]{2,0,1:T(8,128)(2,1)} %copy_bitcast_fusion, s32[1024]{0:T(1024)S(1)} %get-tuple-element.38), kind=kCustom, calls=%fused_computation.4.clone | custom fusion | bytes 5243008 | tf_op jit(solution)/shard_map/while/body/eval_jaxpr/jit(_take)/gather | solution.py:48
  56.7 3.3 %fusion = f32[32,128,128]{2,1,0:T(8,128)S(1)} fusion(bf16[32,320,128]{2,1,0:T(8,128)(2,1)} %gather_fusion.4, bf16[32,320,128]{2,1,0:T(8,128)(2,1)S(1)} %gather_fusion.2, pred[32]{0:T(512)(128)(4,1)S(1)} %get-tuple-element.34, pred[32]{0:T(512)(128)(4,1)S(1)} %get-tuple-element.28), kind=kOutput, calls=%fused_computation.12 | convolution fusion | flops 338165760 | bytes 7340096 | tf_op jit(solution)/shard_map/while/body/eval_jaxpr/rgi,rgj->gij/dot_general | solution.py:49
  60.0 1.6 broadcast_multiply_fusion
  61.6 6.1 %all-to-all-start = ((f32[8,4,128,128]{3,2,1,0:T(8,128)}), f32[8,4,128,128]{3,2,1,0:T(8,128)S(1)}, u32[]{:S(2)}, u32[]{:S(2)}) async-start(f32[8,4,128,128]{3,2,1,0:T(8,128)} %broadcast_multiply_fusion), calls=%async_computation | async-start | bytes 4194304 | tf_op jit(solution)/shard_map/all_to_all | solution.py:57
  67.7 0.2 reduce-scatter.2.cloned.1.call-start
  67.9 0.3 subtract_reduce_fusion
  68.2 0.1 sub.15
  68.3 46.9 %all-to-all-done = f32[8,4,128,128]{3,2,1,0:T(8,128)S(1)} async-done(((f32[8,4,128,128]{3,2,1,0:T(8,128)}), f32[8,4,128,128]{3,2,1,0:T(8,128)S(1)}, u32[]{:S(2)}, u32[]{:S(2)}) %all-to-all-start) | async-done | bytes 2097184 | tf_op jit(solution)/shard_map/all_to_all | solution.py:57
  115.1 3.8 %fusion.7 = f32[32,128,128]{2,0,1:T(8,128)} fusion(s32[32]{0:T(128)S(1)} %sub.15, f32[4,8,128,128]{3,2,1,0:T(8,128)S(1)} %bitcast.45), kind=kOutput, calls=%fused_computation.20 | convolution fusion | flops 201327616 | bytes 4194432 | tf_op jit(solution)/shard_map/dot_general | solution.py:64
  118.9 0.0 reduce-scatter.2.cloned.1.call-update
  118.9 0.1 copy.33
  119.1 0.6 gather_fusion
  119.7 0.1 broadcast_select_fusion.1
  119.8 0.2 slice_reduce_fusion.1
  120.0 0.0 all-gather.3.cloned.1.call-done
  120.0 1.8 %reshape.157 = f32[32,16384]{1,0:T(8,128)S(1)} reshape(f32[524288]{0:T(1024)} %all-gather.3.cloned.1.call-done) | data formatting | bytes 4194304 | tf_op jit(solution)/shard_map/all_gather | solution.py:13
  121.8 0.2 reduce_sum.29
  122.0 0.6 gather_fusion.5
  122.6 0.1 select_multiply_fusion
  122.7 0.1 copy.34
  122.8 0.6 gather_fusion.6
  123.3 0.1 broadcast_select_fusion
  123.4 26.7 %reduce-scatter.2.cloned.1.call-done = f32[8,128,128]{2,0,1:T(8,128)} async-done(((f32[32,128,128]{2,0,1:T(8,128)}), f32[8,128,128]{2,0,1:T(8,128)}) %reduce-scatter.2.cloned.1.call-update) | async-done | bytes 524304 | tf_op jit(solution)/shard_map/reduce_scatter | solution.py:70
  150.1 1.2 multiply_divide_fusion
  151.3 0.9 copy.35
  (16 shorter events, 0.1 us)
Async XLA Ops:
  7.4 37.8 %copy-start = (s32[8,8]{1,0:T(8,128)S(1)}, s32[8,8]{1,0:T(8,128)}, u32[]{:S(2)}) copy-start(s32[8,8]{1,0:T(8,128)} %param.14) | copy-start | bytes 772
  7.4 112.7 %all-gather.3.cloned.1.call-start = ((), (), s32[]{:S(2)}) async-start(), calls=%async_computation.3 | async-start | bytes 2162688 | tf_op jit(solution)/shard_map/all_gather | solution.py:13
  14.2 11.0 %copy-start.2 = (s32[8,8,4]{1,2,0:T(4,128)S(1)}, s32[8,8,4]{1,2,0:T(4,128)}, u32[]{:S(2)}) copy-start(s32[8,8,4]{1,2,0:T(4,128)} %param.13) | copy-start | bytes 3076
  14.2 11.2 %copy-start.3 = (s32[256,2]{0,1:T(2,128)S(1)}, s32[256,2]{0,1:T(2,128)}, u32[]{:S(2)}) copy-start(s32[256,2]{0,1:T(2,128)} %param.15) | copy-start | bytes 6148
  14.2 12.6 %copy-start.1 = (s32[1,128,256]{2,1,0:T(8,128)S(1)}, s32[1,128,256]{2,1,0:T(8,128)}, u32[]{:S(2)}) copy-start(s32[1,128,256]{2,1,0:T(8,128)} %param.12) | copy-start | bytes 393220
  61.6 53.6 %all-to-all-start = ((f32[8,4,128,128]{3,2,1,0:T(8,128)}), f32[8,4,128,128]{3,2,1,0:T(8,128)S(1)}, u32[]{:S(2)}, u32[]{:S(2)}) async-start(f32[8,4,128,128]{3,2,1,0:T(8,128)} %broadcast_multiply_fusion), calls=%async_computation | async-start | bytes 4194304 | tf_op jit(solution)/shard_map/all_to_all | solution.py:57
  67.7 82.4 %reduce-scatter.2.cloned.1.call-start = ((), (), s32[]{:S(2)}) async-start(), calls=%async_computation.2 | async-start | bytes 2621440 | tf_op jit(solution)/shard_map/reduce_scatter | solution.py:70
Sparse Core Ops, SparseCore 0:
  14.3 58.7 all-gather.2
Sparse Core Ops, SparseCore 1:
  119.0 31.0 reduce-scatter.1
